TPU v7x, 32 devices: a whole 2x2x4 slice. The times are simulated.
32 devices in a mesh: space: 8 (over y, x, core), tm: 4 (over z).
Axes of the slice: x: 2, y: 2, z: 4, core: 2. Of those that a mesh axis runs over, the one named last changes fastest.
Arguments:
- vectors: bfloat16 [4, 2, 3, 96, 4096], P('tm', None, None, None, 'space'), may hold values from -6 to 6
- momenta: int32 [2, 3], replicated, may hold values from -3 to 3
- offsets: int32 [8, 3], replicated, may hold values from 0 to 56, as said below
Outputs:
- elementals: float32 [4, 96, 2, 18432], P(None, 'space')
Inputs may be any that keep to these rules, and one draw needn't show every extreme that they name: `offsets`: each row is the corner of one block of 8 x 8 x 8 sites of the 64^3 lattice: its first two coordinates are multiples of 8, its third a multiple of 8; no two rows name the same block, so the blocks never intersect.
All inputs are finite; a program needn't handle non-finite values.
Results may differ from a plain program's by a relative error of at most 0.0055.
Values may be sent and summed in bfloat16 or wider, within the bound.
A program may use at most 128 MiB of HBM per device.

v0:
```python
import math

import jax
import jax.numpy as jnp
from jax import lax
from jax.sharding import PartitionSpec as P

LAT = 64
BRICK = 8
BRICK_Z = 8


def local_coords(site):
    return jnp.stack([site // (BRICK * BRICK_Z), site // BRICK_Z % BRICK, site % BRICK_Z])


def phases(momenta, coords):
    product = jnp.sum(momenta[:, :, None] * coords[None, :, :], axis=1)
    angle = (product % LAT).astype(jnp.float32) * (2.0 * math.pi / LAT)
    return jnp.stack([jnp.cos(angle), jnp.sin(angle)], axis=1)


def complex_term(w_real, w_imag, v_real, v_imag):
    return (w_real * v_real - w_imag * v_imag, w_real * v_imag + w_imag * v_real)


def cross_rows(phase, row_vecs, vecs):
    rows_f = row_vecs.astype(jnp.float32)
    cosine = phase[:, 0][:, None, None, :]
    sine = phase[:, 1][:, None, None, :]
    real_w = cosine * rows_f[0][None] - sine * rows_f[1][None]
    imag_w = cosine * rows_f[1][None] + sine * rows_f[0][None]
    real_w = jnp.transpose(real_w, (2, 0, 1, 3))
    imag_w = jnp.transpose(imag_w, (2, 0, 1, 3))
    real_v = vecs[0].astype(jnp.float32)
    imag_v = vecs[1].astype(jnp.float32)
    real_parts = []
    imag_parts = []
    for colour in range(3):
        first = (colour + 1) % 3
        second = (colour + 2) % 3
        plus_re, plus_im = complex_term(
            real_w[:, :, first, None, :],
            imag_w[:, :, first, None, :],
            real_v[second][None, None],
            imag_v[second][None, None],
        )
        minus_re, minus_im = complex_term(
            real_w[:, :, second, None, :],
            imag_w[:, :, second, None, :],
            real_v[first][None, None],
            imag_v[first][None, None],
        )
        real_parts.append(plus_re - minus_re)
        imag_parts.append(plus_im - minus_im)
    stacked = jnp.stack([jnp.stack(real_parts, axis=3), jnp.stack(imag_parts, axis=3)], axis=3)
    return stacked.astype(jnp.bfloat16)


def mixing(vecs):
    real_v = vecs[0]
    imag_v = vecs[1]
    return jnp.stack([jnp.stack([real_v, imag_v], axis=1), jnp.stack([-imag_v, real_v], axis=1)])


def body(vectors, momenta, offsets):
    local = vectors[0]
    nvec = local.shape[2]
    sites = local.shape[3]
    groups = lax.axis_size("space")
    rows = nvec // groups
    width = 2 * nvec * nvec
    moments = momenta.shape[0]
    mine = lax.axis_index("space") * rows
    empty = jnp.zeros((rows, moments, width), jnp.float32)
    vec_piece = lax.all_gather(local.reshape(6 * nvec, sites), "space", axis=1, tiled=True)
    length = vec_piece.shape[1]
    block = math.gcd(length, sites)

    def advance(index, acc):
        vec_block = lax.dynamic_slice_in_dim(vec_piece, index * block, block, 1).reshape(
            2, 3, nvec, block
        )
        site_ids = index * block + jnp.arange(block, dtype=jnp.int32)
        brick_ids = site_ids // sites
        coords = local_coords(site_ids % sites) + jnp.transpose(
            jnp.take(offsets, brick_ids, axis=0)
        )
        phase_block = phases(momenta, coords)
        row_vecs = lax.dynamic_slice_in_dim(vec_block, mine, rows, 2)
        crossed = cross_rows(phase_block, row_vecs, vec_block)
        part = jnp.einsum(
            "imjqcg,qcrkg->imjrk", crossed, mixing(vec_block), preferred_element_type=jnp.float32
        )
        return acc + part.reshape(rows, moments, width)

    summed = lax.fori_loop(0, length // block, advance, empty)
    finished = summed * (1.0 / math.sqrt(sites * groups))
    gathered = lax.all_gather(finished[None], "tm", axis=0, tiled=True)
    return gathered


def solution(mesh):
    return jax.shard_map(
        body,
        mesh=mesh,
        in_specs=(P("tm", None, None, None, "space"), P(), P()),
        out_specs=P(None, "space", None, None),
        check_vma=False,
    )
```

profile of v0, /device:TPU:0, one launch (start us, length us, event | category | flops | bytes accessed | tf_op | source)
XLA Modules:
  0.0 419.8 jit_solution(16683242958155573261)
XLA Ops:
  8.8 42.8 %all-gather.4.cloned.1.call-done = bf16[576,4096]{1,0:T(8,128)(2,1)} async-done(((bf16[576,512]{1,0:T(8,128)(2,1)}), bf16[576,4096]{1,0:T(8,128)(2,1)}) %all-gather.4.cloned.1.call-update) | async-done | bytes 4718608 | tf_op jit(solution)/shard_map/all_gather | solution.py:76
  51.6 223.0 %while.17 = (s32[]{:T(128)}, f32[12,2,18432]{2,1,0:T(2,128)}, s32[2,3]{0,1:T(4,128)S(1)}, s32[8,3]{1,0:T(8,128)S(1)}, bf16[576,4096]{1,0:T(8,128)(2,1)}, /*index...) while((s32[]{:T(128)}, f32[12,2,18432]{2,1,0:T(2,128)}, ...), condition=%wide.region_2.3_spmd.clone, body=%wide.region_0.2_spmd.clone.sunk | while | flops 2821320704 | bytes 82453736 | solution.py:97
  55.8 7.6 %subtract_convert_fusion.7 = (bf16[12,2,96,1,512]{4,2,3,1,0:T(8,128)(2,1)S(1)}, bf16[12,2,96,1,512]{4,2,3,1,0:T(8,128)(2,1)S(1)}, bf16[12,2,96,1,512]{4,2,3,1,0:...) fusion(f32[96,512]{1,0:T(8,128)S(1)} %get-tuple-element.381, ...), kind=kLoop, calls=%fused_computation.10.clone.1 | loop fusion | flops 56623104 | bytes 15630336 | tf_op jit(solution)/shard_map/convert.7
  71.1 4.2 reshape.462
  83.2 7.6 %subtract_convert_fusion.7 = (bf16[12,2,96,1,512]{4,2,3,1,0:T(8,128)(2,1)S(1)}, bf16[12,2,96,1,512]{4,2,3,1,0:T(8,128)(2,1)S(1)}, bf16[12,2,96,1,512]{4,2,3,1,0:...) fusion(f32[96,512]{1,0:T(8,128)S(1)} %get-tuple-element.381, ...), kind=kLoop, calls=%fused_computation.10.clone.1 | loop fusion | flops 56623104 | bytes 15630336 | tf_op jit(solution)/shard_map/convert.7
  98.5 4.2 reshape.462
  102.6 4.3 %select_add_fusion.2 = f32[12,2,18432]{2,1,0:T(2,128)} fusion(f32[12,2,18432]{2,1,0:T(2,128)} %reshape.462, f32[12,2,18432]{2,1,0:T(2,128)} %get-tuple-element.421, pred[]{:T(512)S(6)} %compare.95), kind=kLoop, calls=%fused_computation.11.clone.1 | loop fusion | flops 884736 | bytes 5308417 | tf_op jit(solution)/shard_map/while/body/eval_jaxpr/add | solution.py:95
  111.1 7.6 %subtract_convert_fusion.7 = (bf16[12,2,96,1,512]{4,2,3,1,0:T(8,128)(2,1)S(1)}, bf16[12,2,96,1,512]{4,2,3,1,0:T(8,128)(2,1)S(1)}, bf16[12,2,96,1,512]{4,2,3,1,0:...) fusion(f32[96,512]{1,0:T(8,128)S(1)} %get-tuple-element.381, ...), kind=kLoop, calls=%fused_computation.10.clone.1 | loop fusion | flops 56623104 | bytes 15630336 | tf_op jit(solution)/shard_map/convert.7
  126.4 4.2 reshape.462
  130.6 4.3 %select_add_fusion.2 = f32[12,2,18432]{2,1,0:T(2,128)} fusion(f32[12,2,18432]{2,1,0:T(2,128)} %reshape.462, f32[12,2,18432]{2,1,0:T(2,128)} %get-tuple-element.421, pred[]{:T(512)S(6)} %compare.95), kind=kLoop, calls=%fused_computation.11.clone.1 | loop fusion | flops 884736 | bytes 5308417 | tf_op jit(solution)/shard_map/while/body/eval_jaxpr/add | solution.py:95
  139.1 7.6 %subtract_convert_fusion.7 = (bf16[12,2,96,1,512]{4,2,3,1,0:T(8,128)(2,1)S(1)}, bf16[12,2,96,1,512]{4,2,3,1,0:T(8,128)(2,1)S(1)}, bf16[12,2,96,1,512]{4,2,3,1,0:...) fusion(f32[96,512]{1,0:T(8,128)S(1)} %get-tuple-element.381, ...), kind=kLoop, calls=%fused_computation.10.clone.1 | loop fusion | flops 56623104 | bytes 15630336 | tf_op jit(solution)/shard_map/convert.7
  154.4 4.2 reshape.462
  158.5 4.3 %select_add_fusion.2 = f32[12,2,18432]{2,1,0:T(2,128)} fusion(f32[12,2,18432]{2,1,0:T(2,128)} %reshape.462, f32[12,2,18432]{2,1,0:T(2,128)} %get-tuple-element.421, pred[]{:T(512)S(6)} %compare.95), kind=kLoop, calls=%fused_computation.11.clone.1 | loop fusion | flops 884736 | bytes 5308417 | tf_op jit(solution)/shard_map/while/body/eval_jaxpr/add | solution.py:95
  167.0 7.6 %subtract_convert_fusion.7 = (bf16[12,2,96,1,512]{4,2,3,1,0:T(8,128)(2,1)S(1)}, bf16[12,2,96,1,512]{4,2,3,1,0:T(8,128)(2,1)S(1)}, bf16[12,2,96,1,512]{4,2,3,1,0:...) fusion(f32[96,512]{1,0:T(8,128)S(1)} %get-tuple-element.381, ...), kind=kLoop, calls=%fused_computation.10.clone.1 | loop fusion | flops 56623104 | bytes 15630336 | tf_op jit(solution)/shard_map/convert.7
  182.3 4.2 reshape.462
  186.4 4.3 %select_add_fusion.2 = f32[12,2,18432]{2,1,0:T(2,128)} fusion(f32[12,2,18432]{2,1,0:T(2,128)} %reshape.462, f32[12,2,18432]{2,1,0:T(2,128)} %get-tuple-element.421, pred[]{:T(512)S(6)} %compare.95), kind=kLoop, calls=%fused_computation.11.clone.1 | loop fusion | flops 884736 | bytes 5308417 | tf_op jit(solution)/shard_map/while/body/eval_jaxpr/add | solution.py:95
  194.9 7.6 %subtract_convert_fusion.7 = (bf16[12,2,96,1,512]{4,2,3,1,0:T(8,128)(2,1)S(1)}, bf16[12,2,96,1,512]{4,2,3,1,0:T(8,128)(2,1)S(1)}, bf16[12,2,96,1,512]{4,2,3,1,0:...) fusion(f32[96,512]{1,0:T(8,128)S(1)} %get-tuple-element.381, ...), kind=kLoop, calls=%fused_computation.10.clone.1 | loop fusion | flops 56623104 | bytes 15630336 | tf_op jit(solution)/shard_map/convert.7
  214.4 4.3 %select_add_fusion.2 = f32[12,2,18432]{2,1,0:T(2,128)} fusion(f32[12,2,18432]{2,1,0:T(2,128)} %reshape.462, f32[12,2,18432]{2,1,0:T(2,128)} %get-tuple-element.421, pred[]{:T(512)S(6)} %compare.95), kind=kLoop, calls=%fused_computation.11.clone.1 | loop fusion | flops 884736 | bytes 5308417 | tf_op jit(solution)/shard_map/while/body/eval_jaxpr/add | solution.py:95
  222.9 7.6 %subtract_convert_fusion.7 = (bf16[12,2,96,1,512]{4,2,3,1,0:T(8,128)(2,1)S(1)}, bf16[12,2,96,1,512]{4,2,3,1,0:T(8,128)(2,1)S(1)}, bf16[12,2,96,1,512]{4,2,3,1,0:...) fusion(f32[96,512]{1,0:T(8,128)S(1)} %get-tuple-element.381, ...), kind=kLoop, calls=%fused_computation.10.clone.1 | loop fusion | flops 56623104 | bytes 15630336 | tf_op jit(solution)/shard_map/convert.7
  242.3 4.3 %select_add_fusion.2 = f32[12,2,18432]{2,1,0:T(2,128)} fusion(f32[12,2,18432]{2,1,0:T(2,128)} %reshape.462, f32[12,2,18432]{2,1,0:T(2,128)} %get-tuple-element.421, pred[]{:T(512)S(6)} %compare.95), kind=kLoop, calls=%fused_computation.11.clone.1 | loop fusion | flops 884736 | bytes 5308417 | tf_op jit(solution)/shard_map/while/body/eval_jaxpr/add | solution.py:95
  250.8 7.6 %subtract_convert_fusion.7 = (bf16[12,2,96,1,512]{4,2,3,1,0:T(8,128)(2,1)S(1)}, bf16[12,2,96,1,512]{4,2,3,1,0:T(8,128)(2,1)S(1)}, bf16[12,2,96,1,512]{4,2,3,1,0:...) fusion(f32[96,512]{1,0:T(8,128)S(1)} %get-tuple-element.381, ...), kind=kLoop, calls=%fused_computation.10.clone.1 | loop fusion | flops 56623104 | bytes 15630336 | tf_op jit(solution)/shard_map/convert.7
  270.3 4.3 %select_add_fusion.2 = f32[12,2,18432]{2,1,0:T(2,128)} fusion(f32[12,2,18432]{2,1,0:T(2,128)} %reshape.462, f32[12,2,18432]{2,1,0:T(2,128)} %get-tuple-element.421, pred[]{:T(512)S(6)} %compare.95), kind=kLoop, calls=%fused_computation.11.clone.1 | loop fusion | flops 884736 | bytes 5308417 | tf_op jit(solution)/shard_map/while/body/eval_jaxpr/add | solution.py:95
  278.2 128.3 %all-gather.6.cloned.1.call-done = f32[48,2,18432]{2,1,0:T(2,128)} async-done(((f32[12,2,18432]{2,1,0:T(2,128)}), f32[48,2,18432]{2,1,0:T(2,128)}) %all-gather.6.cloned.1.call-update) | async-done | bytes 7077904 | tf_op jit(solution)/shard_map/all_gather | solution.py:99
  406.5 6.4 %copy.46 = f32[4,12,2,18432]{3,2,1,0:T(2,128)} copy(f32[4,12,2,18432]{3,2,1,0:T(2,128)} %bitcast.88) | data formatting | bytes 14155776
  (212 shorter events, 115.6 us)
Async XLA Ops:
  6.5 45.1 %all-gather.4.cloned.1.call-start = ((), (), s32[]{:S(2)}) async-start(), calls=%async_computation | async-start | bytes 5308416 | tf_op jit(solution)/shard_map/all_gather | solution.py:76
  7.3 399.3 %all-gather.6.cloned.1.call-start = ((), (), s32[]{:S(2)}) async-start(), calls=%async_computation.1 | async-start | bytes 8847360 | tf_op jit(solution)/shard_map/all_gather | solution.py:99
Sparse Core Ops, SparseCore 0:
  9.2 42.3 all-gather.3
  278.3 128.1 all-gather.5
where the time goes:
time: 421 us; the launch traced here: 420 us
  waiting for transfers between devices  172 us (41%)
  other arithmetic  117 us (28%)
  local copies, waits for them, and re-layouts  84.7 us (20%)
  matrix products  32 us (8%)
  between operations  13.4 us (3%)
    all_gather x1, waiting for transfers between devices, body(): gathered = lax.all_gather(finished[None], 'tm', axis=0, tiled=True)  128 us
    another operation x8, other arithmetic  60.9 us
    all_gather x1, waiting for transfers between devices, body(): lax.all_gather(local.reshape(6 * nvec, sites), 'space', axis=1, tiled=True)  42.8 us
    add x8, other arithmetic, advance(): return acc + part.reshape(rows, moments, width)  34 us
    reshape x8, local copies, waits for them, and re-layouts, advance(): return acc + part.reshape(rows, moments, width)  33.3 us
    dot_general x8, matrix products, advance(): jnp.einsum('imjqcg,qcrkg->imjrk', crossed, mixing(vec_block), preferred_e...  32 us
    dot_general x8, local copies, waits for them, and re-layouts, advance(): jnp.einsum('imjqcg,qcrkg->imjrk', crossed, mixing(vec_block), preferred_e...  14.6 us
    another operation x16, other arithmetic, cross_rows(): jnp.stack([jnp.stack(real_parts, axis=3), jnp.stack(imag_parts, axis=3)],...  13.1 us
  transfers between devices with their start and end apart: 2, of which 2 were waited for; matrix products, arithmetic and copies ran while one was open for 0% of the time, Pallas kernels for 0%

commit v1 on v0

v1 whole, which is shorter than its diff:
```python
import functools
import math

import jax
import jax.numpy as jnp
from jax import lax
from jax.experimental import pallas as pl
from jax.experimental.pallas import tpu as pltpu
from jax.sharding import PartitionSpec as P

LAT = 64
BRICK = 8
BRICK_Z = 8
JB = 32
LANES = 128


def local_coords(site):
    return jnp.stack([site // (BRICK * BRICK_Z), site // BRICK_Z % BRICK, site % BRICK_Z])


def phases(momenta, coords):
    product = jnp.sum(momenta[:, :, None] * coords[None, :, :], axis=1)
    angle = (product % LAT).astype(jnp.float32) * (2.0 * math.pi / LAT)
    return jnp.stack([jnp.cos(angle), jnp.sin(angle)], axis=1)


def compute_kernel(scale, first, seeded, v_ref, row_ref, phase_ref, *refs):
    nvec = v_ref.shape[3]
    sites = v_ref.shape[4]
    rows = row_ref.shape[3]
    moments = phase_ref.shape[1] // 2
    nblocks = nvec // JB
    group = 2 * moments * JB
    if seeded:
        seed_ref, out_ref, row_f, vp_ref = refs[0], refs[1], refs[2], refs[3]
        rest = refs[4:]
        count = len(rest) // 2
        lhs_refs, acc_refs = rest[:count], rest[count:]
    else:
        acc_out, row_f, vp_ref = refs[0], refs[1], refs[2]
        lhs_refs = refs[3:]
        count = len(lhs_refs)
        starts = []
        at = 0
        for n in range(count):
            starts.append(at)
            at += (nblocks - first - n) * group
        acc_refs = [
            acc_out.at[:, pl.ds(starts[n], (nblocks - first - n) * group)] for n in range(count)
        ]
    step = pl.program_id(0)

    @pl.when(step == 0)
    def _():
        at = 0
        for acc in acc_refs:
            wide = acc.shape[1]
            if seeded:
                acc[...] = seed_ref[:, at : at + wide]
            else:
                acc[...] = jnp.zeros(acc.shape, jnp.float32)
            at += wide

    for q in range(2):
        for colour in range(3):
            row_f[q * 3 + colour] = row_ref[0, q, colour].astype(jnp.float32)

    def chunk(index, carry):
        lanes = pl.ds(pl.multiple_of(index * LANES, LANES), LANES)
        for colour in range(3):
            real_v = v_ref[0, 0, colour, :, lanes].astype(jnp.float32)
            imag_v = v_ref[0, 1, colour, :, lanes].astype(jnp.float32)
            for p in range(moments):
                cosine = phase_ref[0, pl.ds(2 * p, 1), lanes]
                sine = phase_ref[0, pl.ds(2 * p + 1, 1), lanes]
                real_x = (cosine * real_v - sine * imag_v).astype(jnp.bfloat16)
                imag_x = (cosine * imag_v + sine * real_v).astype(jnp.bfloat16)
                table = ((real_x, -imag_x), (imag_x, real_x))
                for r in range(2):
                    for q in range(2):
                        at = (colour * 2 + q) * LANES
                        for kb in range(first, nblocks):
                            base = (kb - first) * group + (2 * p + r) * JB
                            vp_ref[base : base + JB, at : at + LANES] = table[r][q][
                                kb * JB : (kb + 1) * JB
                            ]
        for n in range(count):
            jb = first + n
            vecs = [
                [v_ref[0, q, colour, jb * JB : (jb + 1) * JB, lanes] for colour in range(3)]
                for q in range(2)
            ]
            for i in range(rows):
                row = [
                    [
                        jnp.broadcast_to(
                            row_f[q * 3 + colour, pl.ds(i, 1), lanes], (JB, LANES)
                        ).astype(jnp.bfloat16)
                        for colour in range(3)
                    ]
                    for q in range(2)
                ]
                for colour in range(3):
                    a = (colour + 1) % 3
                    b = (colour + 2) % 3
                    real_d = (row[0][a] * vecs[0][b] - row[1][a] * vecs[1][b]) - (
                        row[0][b] * vecs[0][a] - row[1][b] * vecs[1][a]
                    )
                    imag_d = (row[0][a] * vecs[1][b] + row[1][a] * vecs[0][b]) - (
                        row[0][b] * vecs[1][a] + row[1][b] * vecs[0][a]
                    )
                    at = colour * 2 * LANES
                    lhs_refs[n][i * JB : (i + 1) * JB, at : at + LANES] = real_d
                    lhs_refs[n][i * JB : (i + 1) * JB, at + LANES : at + 2 * LANES] = imag_d
            acc_refs[n][...] += lax.dot_general(
                lhs_refs[n][...],
                vp_ref[n * group :, :],
                (((1,), (1,)), ((), ())),
                preferred_element_type=jnp.float32,
            )
        return carry

    lax.fori_loop(0, sites // LANES, chunk, 0)

    if seeded:

        @pl.when(step == pl.num_programs(0) - 1)
        def _():
            at = 0
            for acc in acc_refs:
                wide = acc.shape[1]
                out_ref[:, at : at + wide] = (acc[...] * scale).astype(jnp.bfloat16)
                at += wide


def contract(gathered, row_vecs, phase, scale, first, last, seed, seed_block):
    groups, _, _, nvec, sites = gathered.shape
    rows = row_vecs.shape[3]
    moments = phase.shape[1] // 2
    nblocks = nvec // JB
    group = 2 * moments * JB
    widths = [(nblocks - jb) * group for jb in range(first, last)]
    total = sum(widths)
    depth = 6 * LANES
    seeded = seed is not None
    in_specs = [
        pl.BlockSpec((1, 2, 3, nvec, sites), lambda s: (s, 0, 0, 0, 0)),
        pl.BlockSpec((1, 2, 3, rows, sites), lambda s: (s, 0, 0, 0, 0)),
        pl.BlockSpec((1, 2 * moments, sites), lambda s: (s, 0, 0)),
    ]
    operands = [gathered, row_vecs, phase]
    scratch = [
        pltpu.VMEM((6, rows, sites), jnp.float32),
        pltpu.VMEM((widths[0], depth), jnp.bfloat16),
    ] + [pltpu.VMEM((rows * JB, depth), jnp.bfloat16) for _ in widths]
    if seeded:
        in_specs.append(pl.BlockSpec((rows * JB, total), lambda s: (0, seed_block)))
        operands.append(seed)
        scratch += [pltpu.VMEM((rows * JB, wide), jnp.float32) for wide in widths]
    return pl.pallas_call(
        functools.partial(compute_kernel, scale, first, seeded),
        out_shape=jax.ShapeDtypeStruct(
            (rows * JB, total), jnp.bfloat16 if seeded else jnp.float32
        ),
        grid=(groups,),
        in_specs=in_specs,
        out_specs=pl.BlockSpec((rows * JB, total), lambda s: (0, 0)),
        scratch_shapes=scratch,
        compiler_params=pltpu.CompilerParams(dimension_semantics=("arbitrary",)),
        cost_estimate=pl.CostEstimate(
            flops=2 * groups * sites * 6 * rows * JB * total * 2,
            bytes_accessed=groups * 6 * nvec * sites * 2,
            transcendentals=0,
        ),
        name="contract",
    )(*operands)


def unpack_kernel(rows, moments, nvec, *refs):
    nblocks = nvec // JB
    group = 2 * moments * JB
    pack = LANES // JB
    head_ref, tail_ref, out_ref, full = refs
    tall = full.shape[0] // (rows * moments)
    pieces = []
    for n in range(nblocks):
        source = head_ref if n == 0 else tail_ref
        at = 0 if n == 0 else sum((nblocks - m) * group for m in range(1, n))
        for kb in range(n, nblocks):
            pieces.append((n, kb, source, at))
            at += group
    for jb, kb, source, at in pieces:
        for start in range(0, rows, pack):
            many = min(pack, rows - start)
            block = source[0, start * JB : (start + many) * JB, at : at + group].astype(
                jnp.float32
            )
            turned = -jnp.transpose(block) if jb != kb else None
            for n in range(many):
                for p in range(moments):
                    which = (start + n) * moments + p
                    for r in range(2):
                        lane = (2 * p + r) * JB
                        tile, spot = divmod(r * nvec + kb * JB, LANES)
                        full[
                            which * tall + tile, jb * JB : (jb + 1) * JB, spot : spot + JB
                        ] = block[n * JB : (n + 1) * JB, lane : lane + JB]
                        if jb != kb:
                            tile, spot = divmod(r * nvec + jb * JB, LANES)
                            full[
                                which * tall + tile, kb * JB : (kb + 1) * JB, spot : spot + JB
                            ] = turned[lane : lane + JB, n * JB : (n + 1) * JB]
    wide = 2 * nvec
    tiles = 2 * wide // LANES
    half = nvec // 2
    for which in range(rows * moments):
        parity = []
        for odd in range(2):
            for tile in range(tall):
                line = full[which * tall + tile, pl.ds(odd, half, stride=2), :]
                parity.append(line[:, : min(LANES, wide - tile * LANES)])
        both = jnp.concatenate(parity, axis=1)
        i, p = which // moments, which % moments
        base = i * half * tiles * moments
        for tile in range(tiles):
            out_ref[0, pl.ds(base + tile * moments + p, half, stride=tiles * moments), :] = both[
                :, tile * LANES : (tile + 1) * LANES
            ]


def unpack(head, tail, rows, moments, nvec):
    times = head.shape[0]
    lines = nvec * nvec * 2 // LANES
    flat = pl.pallas_call(
        functools.partial(unpack_kernel, rows, moments, nvec),
        out_shape=jax.ShapeDtypeStruct((times, rows * lines * moments, LANES), jnp.float32),
        grid=(times,),
        in_specs=[
            pl.BlockSpec((1,) + head.shape[1:], lambda t: (t, 0, 0)),
            pl.BlockSpec((1,) + tail.shape[1:], lambda t: (t, 0, 0)),
        ],
        out_specs=pl.BlockSpec((1, rows * lines * moments, LANES), lambda t: (t, 0, 0)),
        scratch_shapes=[
            pltpu.VMEM((rows * moments * -(-2 * nvec // LANES), nvec, LANES), jnp.float32)
        ],
        compiler_params=pltpu.CompilerParams(dimension_semantics=("arbitrary",)),
        name="unpack",
    )(head, tail)
    flat = flat.reshape(times, rows, lines, moments, LANES)
    return jnp.transpose(flat, (0, 1, 3, 2, 4)).reshape(times, rows, moments, lines * LANES)


def body(vectors, momenta, offsets):
    local = vectors[0]
    nvec = local.shape[2]
    sites = local.shape[3]
    groups = lax.axis_size("space")
    rows = nvec // groups
    moments = momenta.shape[0]
    nblocks = nvec // JB
    group = 2 * moments * JB
    mine = lax.axis_index("space") * rows
    half = sites // 2
    site_ids = jnp.arange(sites, dtype=jnp.int32)
    coords = local_coords(site_ids)[:, None, :] + jnp.transpose(offsets)[:, :, None]
    phase = phases(momenta, coords.reshape(3, groups * sites))
    phase = jnp.transpose(phase.reshape(2 * moments, groups, sites), (1, 0, 2))
    scale = 1.0 / math.sqrt(sites * groups)
    early = lax.all_gather(local[..., :half], "space", axis=0)
    late = lax.all_gather(local[..., half:], "space", axis=0)
    early_rows = lax.dynamic_slice_in_dim(early, mine, rows, 3)
    partial = contract(early, early_rows, phase[..., :half], scale, 0, nblocks, None, 0)
    late, partial = lax.optimization_barrier((late, partial))
    late_rows = lax.dynamic_slice_in_dim(late, mine, rows, 3)
    stage = (late, late_rows, phase[..., half:])
    cut = nblocks * group
    seeds = [(partial, 0), (partial, 1)]
    if 2 * cut != partial.shape[1]:
        seeds = [(partial[:, :cut], 0), (partial[:, cut:], 0)]
    head = contract(*stage, scale, 0, 1, *seeds[0])
    head = lax.all_gather(head, "tm", axis=0)
    tail = contract(*stage, scale, 1, nblocks, *seeds[1])
    tail = lax.all_gather(tail, "tm", axis=0)
    return unpack(head, tail, rows, moments, nvec)


def solution(mesh):
    return jax.shard_map(
        body,
        mesh=mesh,
        in_specs=(P("tm", None, None, None, "space"), P(), P()),
        out_specs=P(None, "space", None, None),
        check_vma=False,
    )
```

time: 421 us -> 162 us (0.38)
  other arithmetic: 117 us -> 1.46 us
  waiting for transfers between devices: 172 us -> 85.5 us
  local copies, waits for them, and re-layouts: 84.7 us -> 7.46 us
  Pallas kernels: 0 us -> 53.4 us
  matrix products: 32 us -> 0 us
    all_gather x2 -> x4, waiting for transfers between devices: 171 us -> 84.7 us  [the longest x1 30.9 us: body(): tail = lax.all_gather(tail, 'tm', axis=0)]
    another operation x32 -> x2, other arithmetic: 74.9 us -> 0.04 us  [the longest x1 0.03 us: phases(): return jnp.stack([jnp.cos(angle), jnp.sin(angle)], axis=1)]
    pallas_call x0 -> x4, Pallas kernels: none -> 53.4 us  [the longest x3 45.4 us: contract(): pl.pallas_call(functools.partial(compute_kernel, scale, first, seeded), o...]
    add x16 -> x0, other arithmetic: 34.1 us -> none  [the longest x8 34 us: advance(): return acc + part.reshape(rows, moments, width)]
    reshape x8 -> x2, local copies, waits for them, and re-layouts: 33.3 us -> 0.1 us  [body(): phase = jnp.transpose(phase.reshape(2 * moments, groups, sites), (1, 0, 2))]
    dot_general x8 -> x0, matrix products: 32 us -> none  [advance(): jnp.einsum('imjqcg,qcrkg->imjrk', crossed, mixing(vec_block), preferred_e...]
    dot_general x8 -> x0, local copies, waits for them, and re-layouts: 14.6 us -> none  [advance(): jnp.einsum('imjqcg,qcrkg->imjrk', crossed, mixing(vec_block), preferred_e...]
    gather x16 -> x0, local copies, waits for them, and re-layouts: 9.15 us -> none  [advance(): jnp.take(offsets, brick_ids, axis=0)]
  transfers between devices with their start and end apart: 2 -> 4, of which waited for: 2 -> 4; matrix products, arithmetic and copies ran while one was open for 0% -> 3% of each run, Pallas kernels for 0% -> 21%
where the time goes in v1:
time: 162 us; the launch traced here: 161 us
  waiting for transfers between devices  85.5 us (53%)
  Pallas kernels  53.4 us (33%)
  between operations  13.2 us (8%)
  local copies, waits for them, and re-layouts  7.46 us (5%)
    pallas_call x3, Pallas kernels, contract(): pl.pallas_call(functools.partial(compute_kernel, scale, first, seeded), o...  45.4 us
    all_gather x1, waiting for transfers between devices, body(): tail = lax.all_gather(tail, 'tm', axis=0)  30.9 us
    all_gather x1, waiting for transfers between devices, body(): early = lax.all_gather(local[..., :half], 'space', axis=0)  28.5 us
    all_gather x1, waiting for transfers between devices, body(): head = lax.all_gather(head, 'tm', axis=0)  15.6 us
    all_gather x1, waiting for transfers between devices, body(): late = lax.all_gather(local[..., half:], 'space', axis=0)  9.66 us
    pallas_call x1, Pallas kernels, unpack(): pl.pallas_call(functools.partial(unpack_kernel, rows, moments, nvec), out...  8 us
  transfers between devices with their start and end apart: 4, of which 4 were waited for; matrix products, arithmetic and copies ran while one was open for 3% of the time, Pallas kernels for 21%

profile of v1, /device:TPU:0, one launch (start us, length us, event | category | flops | bytes accessed | tf_op | source)
XLA Modules:
  0.0 161.1 jit_solution(8468818117489288448)
XLA Ops:
  6.5 1.9 %fusion.6 = (bf16[2,3,96,256]{3,2,1,0:T(8,128)(2,1)}, bf16[2,3,96,256]{3,2,1,0:T(8,128)(2,1)}) fusion(bf16[2,3,96,512]{3,2,1,0:T(8,128)(2,1)} %bitcast.25), kind=kLoop, calls=%fused_computation.27 | loop fusion | bytes 1179648 | tf_op jit(solution)/shard_map/slice | solution.py:270
  8.4 0.0 all-gather.11.cloned.1.call-update
  8.5 0.0 all-gather.9.cloned.1.call-start
  8.5 0.7 all-gather.9.cloned.1.call-update
  9.2 0.0 all-gather.13.cloned.1.call-start
  9.3 0.8 copy.9
  10.1 0.8 add_bitcast_fusion
  10.9 0.1 multiply_reduce_fusion
  11.0 0.5 fusion.4
  11.6 0.1 copy.10
  11.6 0.1 reshape.187
  11.7 0.6 fusion.7
  12.4 28.5 %all-gather.11.cloned.1.call-done = bf16[16,3,96,256]{3,2,1,0:T(8,128)(2,1)} async-done(((bf16[2,3,96,256]{3,2,1,0:T(8,128)(2,1)}), bf16[16,3,96,256]{3,2,1,0:T(8,128)(2,1)}) %all-gather.11.cloned.1.call-update) | async-done | bytes 2359312 | tf_op jit(solution)/shard_map/all_gather | solution.py:270
  40.9 2.0 %constant_dynamic-slice_fusion.1.row_ref = bf16[8,2,3,12,256]{4,3,2,1,0:T(8,128)(2,1)} fusion(bf16[8,2,3,96,256]{4,3,2,1,0:T(8,128)(2,1)} %bitcast.31, s32[]{:T(128)S(6)} %select_n.68), kind=kLoop, calls=%fused_computation.26 | loop fusion | bytes 589828 | tf_op jit(solution)/shard_map/dynamic_slice | solution.py:272
  42.8 19.1 %contract.3.refs_0_ = f32[384,768]{1,0:T(8,128)} custom-call(bf16[8,2,3,96,256]{4,3,2,1,0:T(8,128)(2,1)} %bitcast.32, bf16[8,2,3,12,256]{4,3,2,1,0:T(8,128)(2,1)} %constant_dynamic-slice_fusion.1.row_ref, f32[8,4,256]{2,1,0:T(4,128)} %get-tuple-element.12.phase_ref), custom_call_target="tpu_custom_call" | custom-call | flops 14495514624 | bytes 2359296 | tf_op jit(solution)/shard_map/contract/pallas_call | solution.py:161
  62.0 9.7 %all-gather.9.cloned.1.call-done = bf16[16,3,96,256]{3,2,1,0:T(8,128)(2,1)} async-done(((bf16[2,3,96,256]{3,2,1,0:T(8,128)(2,1)}), bf16[16,3,96,256]{3,2,1,0:T(8,128)(2,1)}) %all-gather.9.cloned.1.call-update) | async-done | bytes 2359312 | tf_op jit(solution)/shard_map/all_gather | solution.py:271
  71.7 2.0 %constant_dynamic-slice_fusion.row_ref = bf16[8,2,3,12,256]{4,3,2,1,0:T(8,128)(2,1)} fusion(bf16[8,2,3,96,256]{4,3,2,1,0:T(8,128)(2,1)} %bitcast.28, s32[]{:T(128)S(6)} %select_n.68), kind=kLoop, calls=%fused_computation.25 | loop fusion | bytes 589828 | tf_op jit(solution)/shard_map/dynamic_slice | solution.py:275
  73.6 11.6 %contract.4 = bf16[384,384]{1,0:T(8,128)(2,1)} custom-call(bf16[8,2,3,96,256]{4,3,2,1,0:T(8,128)(2,1)} %bitcast.29, bf16[8,2,3,12,256]{4,3,2,1,0:T(8,128)(2,1)} %constant_dynamic-slice_fusion.row_ref, f32[8,4,256]{2,1,0:T(4,128)} %get-tuple-element.11.phase_ref, f32[384,768]{1,0:T(8,128)} %contract.3.refs_0_), custom_call_target="tpu_custom_call" | custom-call | flops 7247757312 | bytes 2359296 | tf_op jit(solution)/shard_map/contract/pallas_call | solution.py:161
  85.2 0.0 all-gather.15.cloned.1.call-start
  85.3 14.7 %contract.5 = bf16[384,384]{1,0:T(8,128)(2,1)} custom-call(bf16[8,2,3,96,256]{4,3,2,1,0:T(8,128)(2,1)} %bitcast.30, bf16[8,2,3,12,256]{4,3,2,1,0:T(8,128)(2,1)} %constant_dynamic-slice_fusion.row_ref, f32[8,4,256]{2,1,0:T(4,128)} %get-tuple-element.11.phase_ref, f32[384,768]{1,0:T(8,128)} %contract.3.refs_0_), custom_call_target="tpu_custom_call" | custom-call | flops 7247757312 | bytes 2359296 | tf_op jit(solution)/shard_map/contract/pallas_call | solution.py:161
  100.0 0.0 all-gather.15.cloned.1.call-update
  100.0 15.6 %all-gather.13.cloned.1.call-done = bf16[1536,384]{1,0:T(8,128)(2,1)} async-done(((bf16[384,384]{1,0:T(8,128)(2,1)}), bf16[1536,384]{1,0:T(8,128)(2,1)}) %all-gather.13.cloned.1.call-update) | async-done | bytes 1179664 | tf_op jit(solution)/shard_map/all_gather | solution.py:282
  115.7 30.9 %all-gather.15.cloned.1.call-done = bf16[1536,384]{1,0:T(8,128)(2,1)} async-done(((bf16[384,384]{1,0:T(8,128)(2,1)}), bf16[1536,384]{1,0:T(8,128)(2,1)}) %all-gather.15.cloned.1.call-update) | async-done | bytes 1179664 | tf_op jit(solution)/shard_map/all_gather | solution.py:284
  146.6 8.0 %unpack.1 = f32[4,3456,128]{2,1,0:T(8,128)} custom-call(bf16[4,384,384]{2,1,0:T(8,128)(2,1)} %bitcast.23, bf16[4,384,384]{2,1,0:T(8,128)(2,1)} %bitcast.24), custom_call_target="tpu_custom_call" | custom-call | tf_op jit(solution)/shard_map/unpack/pallas_call | solution.py:235
  (8 shorter events, 0.2 us)
Async XLA Ops:
  6.5 34.3 %all-gather.11.cloned.1.call-start = ((), (), s32[]{:S(2)}) async-start(), calls=%async_computation.1 | async-start | bytes 2654208 | tf_op jit(solution)/shard_map/all_gather | solution.py:270
  8.5 63.2 %all-gather.9.cloned.1.call-start = ((), (), s32[]{:S(2)}) async-start(), calls=%async_computation | async-start | bytes 2654208 | tf_op jit(solution)/shard_map/all_gather | solution.py:271
  9.2 106.4 %all-gather.13.cloned.1.call-start = ((), (), s32[]{:S(2)}) async-start(), calls=%async_computation.2 | async-start | bytes 1474560 | tf_op jit(solution)/shard_map/all_gather | solution.py:282
  85.2 61.4 %all-gather.15.cloned.1.call-start = ((), (), s32[]{:S(2)}) async-start(), calls=%async_computation.3 | async-start | bytes 1474560 | tf_op jit(solution)/shard_map/all_gather | solution.py:284
Sparse Core Ops, SparseCore 0:
  9.2 31.5 all-gather.10
  42.7 28.8 all-gather.8
  85.4 30.2 all-gather.12
  117.1 29.4 all-gather.14
